TPU v7x, 256 devices: a whole 4x4x8 slice. The times are simulated.
256 devices in a mesh: row: 16 (over z, x_lo), col: 16 (over x_hi, y, core).
Axes of the slice: x: 4 (x_hi: 2, x_lo: 2; x = x_hi * 2 + x_lo), y: 4, z: 8, core: 2. Of those that a mesh axis runs over, the one named last changes fastest.
Arguments:
- field: bfloat16 [128, 2048, 2048], P(None, 'row', 'col'), may hold values from -6 to 6
- solid_flags: int32 [128, 256, 128], P(None, 'row', 'col'), may hold values 0 or 1
- deriv_matrix: bfloat16 [2048, 2048], replicated, may hold values from -0.125 to 0.125
Outputs:
- filtered: bfloat16 [128, 2048, 2048], P('col', 'row')
- deriv_z: bfloat16 [128, 2048, 2048], P('col', 'row')
Inputs may be any that keep to these rules, and one draw needn't show every extreme that they name: `solid_flags`: 1 marks a solid block, 0 a fluid one.
All inputs are finite; a program needn't handle non-finite values.
Results may differ from a plain program's by a relative error of at most 0.0058.
Values may be sent and summed in bfloat16 or wider, within the bound.
A program may use at most 64 MiB of HBM per device.

v0:
```python
import jax
import jax.numpy as jnp
from jax import lax
from jax.sharding import PartitionSpec as P

YBLK = 8
ZBLK = 16


filter_taps = ((-3, 1.0), (-2, -6.0), (-1, 15.0), (0, -20.0), (1, 15.0), (2, -6.0), (3, 1.0))


def with_halo(block, sides, width):
    for axis, dim in sides:
        count = lax.axis_size(axis)
        forward = [(i, i + 1) for i in range(count - 1)]
        forward.append((count - 1, 0))
        backward = [(target, source) for source, target in forward]
        low = lax.ppermute(
            lax.slice_in_dim(block, block.shape[dim] - width, None, axis=dim), axis, forward
        )
        high = lax.ppermute(lax.slice_in_dim(block, 0, width, axis=dim), axis, backward)
        block = jnp.concatenate([low, block, high], axis=dim)
    return block


def grouped_exchange(shard, axis, split_dim, concat_dim, work, item_dim, out_dim):
    items = jax.tree.leaves(shard)[0].shape[item_dim]
    count = 2 if items % 2 == 0 else 1
    done = []
    for k in range(count):
        group = jax.tree.map(
            lambda a: lax.slice_in_dim(
                a, k * (items // count), (k + 1) * (items // count), axis=item_dim
            ),
            shard,
        )
        done.append(
            work(
                lax.all_to_all(
                    group, axis, split_axis=split_dim, concat_axis=concat_dim, tiled=True
                )
            )
        )
    return jax.tree.map(lambda *parts: jnp.concatenate(parts, axis=out_dim), *done)


def smooth_padded(padded, axis, length):
    center = lax.slice_in_dim(padded, 3, 3 + length, axis=axis).astype(jnp.float32)
    total = center
    for offset, tap in filter_taps:
        shifted = lax.slice_in_dim(padded, 3 + offset, 3 + offset + length, axis=axis)
        total = total + tap / 64.0 * shifted.astype(jnp.float32)
    return total


def shards(field, solid_flags, deriv_matrix):
    xcount, ycount, zcount = field.shape
    blocks = solid_flags.astype(jnp.float32)
    nyb = blocks.shape[1]
    nzb = blocks.shape[2]
    solid = jnp.broadcast_to(blocks[:, :, None, :, None], (xcount, nyb, YBLK, nzb, ZBLK)).reshape(
        xcount, ycount, zcount
    )
    masked = (field.astype(jnp.float32) * (1.0 - solid)).astype(jnp.bfloat16)
    ypadded = with_halo(masked, (("row", 1),), 3)
    yfilt = smooth_padded(ypadded, 1, ycount).astype(jnp.bfloat16)

    def prepare(lines):
        full = lines.shape[2]
        padded = jnp.concatenate([lines[:, :, full - 3 :], lines, lines[:, :, :3]], axis=2)
        return smooth_padded(padded, 2, full).astype(jnp.bfloat16)

    def finish(lines):
        ready = prepare(lines)
        flat = ready.reshape(-1, ready.shape[2])
        deriv = jnp.dot(flat, deriv_matrix, preferred_element_type=jnp.float32).astype(jnp.bfloat16)
        return (ready, deriv.reshape(ready.shape))

    filtered, deriv_z = grouped_exchange(yfilt, "col", 0, 2, finish, 1, 1)
    return (filtered, deriv_z)


def solution(mesh):
    in_specs = (P(None, "row", "col"), P(None, "row", "col"), P())
    out_specs = (P("col", "row", None), P("col", "row", None))
    return jax.shard_map(shards, mesh=mesh, in_specs=in_specs, out_specs=out_specs, check_vma=False)
```

profile of v0, /device:TPU:1, one launch (start us, length us, event | category | flops | bytes accessed | tf_op | source)
XLA Modules:
  0.0 135.2 jit_solution(9472462184685314685)
XLA Ops:
  0.6 0.8 convert_subtract_fusion
  1.5 6.9 %copy.19 = bf16[128,128,128]{0,2,1:T(8,128)(2,1)} copy(bf16[128,128,128]{2,1,0:T(8,128)(2,1)} %param.3) | data formatting | bytes 8388608 | tf_op args[0]
  8.4 0.9 broadcast_in_dim.2
  9.3 3.5 %multiply_convert_fusion = bf16[128,128,128]{0,2,1:T(8,128)(2,1)S(1)} fusion(f32[128,128,128]{0,2,1:T(8,128)S(1)} %bitcast.23, bf16[128,128,128]{0,2,1:T(8,128)(2,1)} %copy.19), kind=kLoop, calls=%fused_computation.9 | loop fusion | flops 6291456 | bytes 16777216 | tf_op jit(solution)/shard_map/convert_element_type | solution.py:65
  12.8 2.1 %collective-permute-start = (bf16[128,3,128]{0,2,1:T(8,128)(2,1)S(1)}, bf16[128,3,128]{0,2,1:T(8,128)(2,1)S(1)}, u32[]{:S(2)}, u32[]{:S(2)}) collective-permute-start(bf16[128,3,128]{0,2,1:T(8,128)(2,1)S(1)} %get-tuple-element.4), channel_id=1, source_target_pairs={{0,16},{16,32},{32,48},{48,64},{64,80},{80,96},{96,112},{112,128},... | collective-permute-start | bytes 294920 | tf_op jit(solution)/shard_map/ppermute | solution.py:19
  14.9 5.4 %collective-permute-start.1 = (bf16[128,3,128]{0,2,1:T(8,128)(2,1)S(1)}, bf16[128,3,128]{0,2,1:T(8,128)(2,1)S(1)}, u32[]{:S(2)}, u32[]{:S(2)}) collective-permute-start(bf16[128,3,128]{0,2,1:T(8,128)(2,1)S(1)} %get-tuple-element.5), channel_id=1, source_target_pairs={{16,0},{32,16},{48,32},{64,48},{80,64},{96,80},{112,96},{128,112},... | collective-permute-start | bytes 294920 | tf_op jit(solution)/shard_map/ppermute | solution.py:22
  20.3 2.4 %collective-permute-done = bf16[128,3,128]{0,2,1:T(8,128)(2,1)S(1)} collective-permute-done((bf16[128,3,128]{0,2,1:T(8,128)(2,1)S(1)}, bf16[128,3,128]{0,2,1:T(8,128)(2,1)S(1)}, u32[]{:S(2)}, u32[]{:S(2)}) %collective-permute-start) | collective-permute-done | bytes 98336 | tf_op jit(solution)/shard_map/ppermute | solution.py:19
  22.7 0.0 collective-permute-done.1
  22.7 7.6 %fusion.6 = bf16[128,128,128]{0,2,1:T(8,128)(2,1)S(1)} fusion(bf16[128,128,128]{0,2,1:T(8,128)(2,1)S(1)} %multiply_convert_fusion, bf16[128,3,128]{0,2,1:T(8,128)(2,1)S(1)} %collective-permute-done.1, bf16[128,3,128]{0,2,1:T(8,128)(2,1)S(1)} %collective-permute-done), kind=kLoop, calls=%fused_computation.8 | loop fusion | flops 58720256 | bytes 8585216 | tf_op jit(solution)/shard_map/convert_element_type | solution.py:67
  30.3 1.6 %fusion.33 = (bf16[128,64,128]{0,2,1:T(8,128)(2,1)S(1)}, bf16[128,64,128]{0,2,1:T(8,128)(2,1)}) fusion(bf16[128,128,128]{0,2,1:T(8,128)(2,1)S(1)} %fusion.6), kind=kLoop, calls=%fused_computation.65 | loop fusion | bytes 8388608 | tf_op jit(solution)/shard_map/slice | solution.py:33
  31.9 2.8 %copy.20 = bf16[128,64,128]{2,1,0:T(8,128)(2,1)} copy(bf16[128,64,128]{0,2,1:T(8,128)(2,1)S(1)} %get-tuple-element.2) | data formatting | bytes 4194304 | tf_op jit(solution)/shard_map/slice | solution.py:33
  34.6 7.9 %all-to-all-start = ((bf16[128,64,128]{2,1,0:T(8,128)(2,1)}), bf16[128,64,128]{2,1,0:T(8,128)(2,1)S(1)}, u32[]{:S(2)}, u32[]{:S(2)}) async-start(bf16[128,64,128]{2,1,0:T(8,128)(2,1)} %copy.20), calls=%async_computation | async-start | bytes 4194304 | tf_op jit(solution)/shard_map/all_to_all | solution.py:40
  42.5 4.1 %copy.22 = bf16[128,64,128]{2,1,0:T(8,128)(2,1)} copy(bf16[128,64,128]{0,2,1:T(8,128)(2,1)} %get-tuple-element.3) | data formatting | bytes 4194304 | tf_op jit(solution)/shard_map/slice | solution.py:33
  46.7 24.2 %all-to-all-done = bf16[128,64,128]{2,1,0:T(8,128)(2,1)S(1)} async-done(((bf16[128,64,128]{2,1,0:T(8,128)(2,1)}), bf16[128,64,128]{2,1,0:T(8,128)(2,1)S(1)}, u32[]{:S(2)}, u32[]{:S(2)}) %all-to-all-start) | async-done | bytes 2097184 | tf_op jit(solution)/shard_map/all_to_all | solution.py:40
  70.9 0.0 copy-start
  70.9 6.9 %all-to-all-start.1 = ((bf16[128,64,128]{2,1,0:T(8,128)(2,1)}), bf16[128,64,128]{2,1,0:T(8,128)(2,1)}, u32[]{:S(2)}, u32[]{:S(2)}) async-start(bf16[128,64,128]{2,1,0:T(8,128)(2,1)} %copy.22), calls=%async_computation.1 | async-start | bytes 4194304 | tf_op jit(solution)/shard_map/all_to_all | solution.py:40
  77.8 0.0 copy-done
  77.8 2.2 %copy.29 = bf16[16,8,8,8,128]{4,3,0,2,1:T(8,128)(2,1)S(1)} copy(bf16[16,8,8,8,128]{4,3,2,1,0:T(8,128)(2,1)} %bitcast.28) | data formatting | bytes 4194304 | tf_op jit(solution)/shard_map/all_to_all | solution.py:40
  80.0 0.1 fusion.35
  80.1 26.2 %all-to-all-done.1 = bf16[128,64,128]{2,1,0:T(8,128)(2,1)} async-done(((bf16[128,64,128]{2,1,0:T(8,128)(2,1)}), bf16[128,64,128]{2,1,0:T(8,128)(2,1)}, u32[]{:S(2)}, u32[]{:S(2)}) %all-to-all-start.1) | async-done | bytes 2097184 | tf_op jit(solution)/shard_map/all_to_all | solution.py:40
  106.3 0.0 slice-start
  106.3 2.3 %copy.28 = bf16[16,8,8,8,128]{4,3,0,2,1:T(8,128)(2,1)S(1)} copy(bf16[16,8,8,8,128]{4,3,2,1,0:T(8,128)(2,1)} %bitcast.13) | data formatting | bytes 4194304 | tf_op jit(solution)/shard_map/all_to_all | solution.py:40
  108.6 0.1 fusion.36
  108.7 0.0 slice-start.1
  108.7 11.9 %fusion.13 = (bf16[8,64,2048]{2,1,0:T(8,128)(2,1)S(1)}, bf16[8,64,2048]{2,1,0:T(8,128)(2,1)S(1)}) fusion(bf16[8,64,2048]{2,1,0:T(8,128)(2,1)S(1)} %bitcast.25, bf16[8,64,3]{2,1,0:T(8,128)(2,1)S(1)} %get-tuple-element.7, bf16[8,64,3]{2,1,0:T(8,128)(2,1)S(1)} %get-tuple-element.6, bf16[8,64,3]{2,1,0:T(8,128)(2,1)S(1)} %get-tuple-element.9, ...), kind=kLoop, calls=%fused_computation.24 | loop fusion | flops 83886080 | bytes 8400896 | tf_op jit(solution)/shard_map/convert_element_type | solution.py:72
  120.6 2.6 %pad_maximum_fusion.2 = bf16[8,128,2048]{2,1,0:T(8,128)(2,1)} fusion(bf16[8,64,2048]{2,1,0:T(8,128)(2,1)S(1)} %get-tuple-element.11, bf16[8,64,2048]{2,1,0:T(8,128)(2,1)S(1)} %get-tuple-element.10), kind=kLoop, calls=%fused_computation.38 | loop fusion | flops 8388608 | bytes 8388608 | tf_op jit(solution)/shard_map/concatenate | solution.py:45
  123.2 0.0 slice-done
  123.2 0.0 slice-done.1
  123.2 4.7 %convolution_convert_fusion.1 = bf16[512,2048]{1,0:T(8,128)(2,1)S(1)} fusion(bf16[512,2048]{1,0:T(8,128)(2,1)S(1)} %bitcast.30, bf16[2048,2048]{1,0:T(8,128)(2,1)S(1)} %bitcast.34), kind=kOutput, calls=%fused_computation.49 | convolution fusion | flops 4296015872 | bytes 12582912 | tf_op jit(solution)/shard_map/dot_general | solution.py:77
  127.9 4.7 %convolution_convert_fusion = bf16[512,2048]{1,0:T(8,128)(2,1)S(1)} fusion(bf16[512,2048]{1,0:T(8,128)(2,1)S(1)} %bitcast.29, bf16[2048,2048]{1,0:T(8,128)(2,1)S(1)} %bitcast.34), kind=kOutput, calls=%fused_computation.48 | convolution fusion | flops 4296015872 | bytes 12582912 | tf_op jit(solution)/shard_map/dot_general | solution.py:77
  132.6 2.6 %pad_maximum_fusion.3 = bf16[8,128,2048]{2,1,0:T(8,128)(2,1)} fusion(bf16[8,64,2048]{2,1,0:T(8,128)(2,1)S(1)} %bitcast.32, bf16[8,64,2048]{2,1,0:T(8,128)(2,1)S(1)} %bitcast.31), kind=kLoop, calls=%fused_computation.39 | loop fusion | flops 8388608 | bytes 8388608 | tf_op jit(solution)/shard_map/concatenate | solution.py:45
  (2 shorter events, 0.0 us)
Async XLA Ops:
  12.8 9.9 %collective-permute-start = (bf16[128,3,128]{0,2,1:T(8,128)(2,1)S(1)}, bf16[128,3,128]{0,2,1:T(8,128)(2,1)S(1)}, u32[]{:S(2)}, u32[]{:S(2)}) collective-permute-start(bf16[128,3,128]{0,2,1:T(8,128)(2,1)S(1)} %get-tuple-element.4), channel_id=1, source_target_pairs={{0,16},{16,32},{32,48},{48,64},{64,80},{80,96},{96,112},{112,128},... | collective-permute-start | bytes 294920 | tf_op jit(solution)/shard_map/ppermute | solution.py:19
  14.9 7.8 %collective-permute-start.1 = (bf16[128,3,128]{0,2,1:T(8,128)(2,1)S(1)}, bf16[128,3,128]{0,2,1:T(8,128)(2,1)S(1)}, u32[]{:S(2)}, u32[]{:S(2)}) collective-permute-start(bf16[128,3,128]{0,2,1:T(8,128)(2,1)S(1)} %get-tuple-element.5), channel_id=1, source_target_pairs={{16,0},{32,16},{48,32},{64,48},{80,64},{96,80},{112,96},{128,112},... | collective-permute-start | bytes 294920 | tf_op jit(solution)/shard_map/ppermute | solution.py:22
  34.6 36.2 %all-to-all-start = ((bf16[128,64,128]{2,1,0:T(8,128)(2,1)}), bf16[128,64,128]{2,1,0:T(8,128)(2,1)S(1)}, u32[]{:S(2)}, u32[]{:S(2)}) async-start(bf16[128,64,128]{2,1,0:T(8,128)(2,1)} %copy.20), calls=%async_computation | async-start | bytes 4194304 | tf_op jit(solution)/shard_map/all_to_all | solution.py:40
  70.9 6.9 %copy-start = (bf16[128,64,128]{2,1,0:T(8,128)(2,1)}, bf16[128,64,128]{2,1,0:T(8,128)(2,1)S(1)}, u32[]{:S(2)}) copy-start(bf16[128,64,128]{2,1,0:T(8,128)(2,1)S(1)} %all-to-all-done) | copy-start | bytes 6291460
  70.9 35.4 %all-to-all-start.1 = ((bf16[128,64,128]{2,1,0:T(8,128)(2,1)}), bf16[128,64,128]{2,1,0:T(8,128)(2,1)}, u32[]{:S(2)}, u32[]{:S(2)}) async-start(bf16[128,64,128]{2,1,0:T(8,128)(2,1)} %copy.22), calls=%async_computation.1 | async-start | bytes 4194304 | tf_op jit(solution)/shard_map/all_to_all | solution.py:40
  106.3 16.9 %slice-start = ((s8[8388608]{0:T(1024)(128)(4,1)}), s8[4194304]{0:T(1024)(128)(4,1)S(1)}, s32[]{:S(2)}) async-start(s8[8388608]{0:T(1024)(128)(4,1)} %bitcast.33), calls=%async_computation.2 | async-start | bytes 8388608
  108.7 14.5 %slice-start.1 = ((s8[8388608]{0:T(1024)(128)(4,1)}), s8[4194304]{0:T(1024)(128)(4,1)S(1)}, s32[]{:S(2)}) async-start(s8[8388608]{0:T(1024)(128)(4,1)} %bitcast.33), calls=%async_computation.3 | async-start | bytes 8388608
where the time goes:
time: 137 us; the launch traced here: 135 us
  waiting for transfers between devices  52.8 us (39%)
  other arithmetic  29 us (21%)
  starting transfers between devices  22.3 us (16%)
  local copies, waits for them, and re-layouts  21 us (15%)
  matrix products  9.39 us (7%)
    all_to_all x2, waiting for transfers between devices, grouped_exchange(): lax.all_to_all(group, axis, split_axis=split_dim, concat_axis=concat_dim,...  50.4 us
    all_to_all x2, starting transfers between devices, grouped_exchange(): lax.all_to_all(group, axis, split_axis=split_dim, concat_axis=concat_dim,...  14.8 us
    convert_element_type x1, other arithmetic, prepare(): return smooth_padded(padded, 2, full).astype(jnp.bfloat16)  11.9 us
    dot_general x2, matrix products, finish(): jnp.dot(flat, deriv_matrix, preferred_element_type=jnp.float32)  9.39 us
    slice x3, local copies, waits for them, and re-layouts, grouped_exchange(): lax.slice_in_dim(a, k * (items // count), (k + 1) * (items // count), axi...  8.5 us
    convert_element_type x1, other arithmetic, shards(): yfilt = smooth_padded(ypadded, 1, ycount).astype(jnp.bfloat16)  7.55 us
    unnamed x7, local copies, waits for them, and re-layouts  6.91 us
    ppermute x1, starting transfers between devices, with_halo(): lax.ppermute(lax.slice_in_dim(block, 0, width, axis=dim), axis, backward)  5.38 us
  transfers between devices with their start and end apart: 4, of which 3 were waited for; matrix products, arithmetic and copies ran while one was open for 5% of the time, Pallas kernels for 0%

commit v1 on v0

v1 whole, which is shorter than its diff:
```python
import functools

import jax
import jax.numpy as jnp
import numpy as np
from jax import lax
from jax.experimental import pallas as pl
from jax.experimental.pallas import tpu as pltpu
from jax.sharding import PartitionSpec as P

MESH = pl.DeviceIdType.MESH
YBLK = 8
ZBLK = 16
TAPS = {-3: 1.0, -2: -6.0, -1: 15.0, 0: 44.0, 1: 15.0, 2: -6.0, 3: 1.0}


def y_matrix(ny):
    out = np.zeros((ny, ny), np.float32)
    for r in range(ny):
        for o, tap in TAPS.items():
            if 0 <= r + o < ny:
                out[r, r + o] = tap / 64.0
    return out


def halo_matrix(lines):
    up = np.zeros((lines * 3, lines * 16), np.float32)
    down = np.zeros((lines * 3, lines * 16), np.float32)
    for l in range(lines):
        for j in range(3):
            for q in range(3):
                o = q - (j - 3)
                if o in TAPS:
                    up[l * 3 + j, l * 16 + q] = TAPS[o] / 64.0
                o = (q - 3) - j
                if o in TAPS:
                    down[l * 3 + j, l * 16 + 8 + 5 + q] = TAPS[o] / 64.0
    return np.concatenate([up, down], axis=0)


def spread_matrix(lines):
    out = np.zeros((lines * 16, lines * 6), np.float32)
    for l in range(lines):
        for j in range(3):
            out[l * 16 + 8 + 5 + j, l * 3 + j] = 1.0
            out[l * 16 + j, lines * 3 + l * 3 + j] = 1.0
    return out


def z_matrix(nz):
    out = np.zeros((4 * nz, 2 * nz), np.float32)
    for c in range(2 * nz):
        for o, tap in TAPS.items():
            out[nz + c + o, c] = tap / 64.0
    return out


def expand_matrix(nzb):
    return np.repeat(np.eye(nzb, dtype=np.float32), ZBLK, axis=1)


def exchange_kernel(
    nrow, ncol, order,
    field, flags_in, dmat, fy_in, ch_in, sp_in, bz_in, ex_in,
    filt, der, tail, dv,
    fbuf, etop, ebot, mask, ybuf, recv, hup, hdown, hfrom_next, hfrom_prev, edges, fy, ch, sp, bz, ex, flags,
    in_sem, fsem, send_sem, recv_sem, hsend_sem, hrecv_sem,
):
    row, col = lax.axis_index("row"), lax.axis_index("col")
    above, below = lax.rem(row + nrow - 1, nrow), lax.rem(row + 1, nrow)
    lines, ny, nz = fbuf.shape[0], fbuf.shape[2], fbuf.shape[3]
    nyb = flags.shape[0]

    flag_loads = [
        pltpu.make_async_copy(flags_in, flags, in_sem.at[7]),
        pltpu.make_async_copy(ex_in, ex, in_sem.at[8]),
    ]
    for copy in flag_loads:
        copy.start()
    loads = [
        pltpu.make_async_copy(field.at[:, :, pl.ds(0, 8), :], etop, in_sem.at[0]),
        pltpu.make_async_copy(field.at[:, :, pl.ds(ny - 8, 8), :], ebot, in_sem.at[1]),
        pltpu.make_async_copy(ch_in, ch, in_sem.at[2]),
        pltpu.make_async_copy(fy_in, fy, in_sem.at[3]),
    ]
    for copy in loads:
        copy.start()
    field_loads = [pltpu.make_async_copy(field.at[:, k], fbuf.at[k], fsem.at[k]) for k in range(lines)]
    for copy in field_loads:
        copy.start()
    late = [
        pltpu.make_async_copy(sp_in, sp, in_sem.at[4]),
        pltpu.make_async_copy(bz_in, bz, in_sem.at[5]),
        pltpu.make_async_copy(dmat, dv, in_sem.at[6]),
    ]
    for copy in late:
        copy.start()

    barrier = pltpu.get_barrier_semaphore()
    for s in range(1, ncol):
        pl.semaphore_signal(
            barrier, inc=1, device_id={"row": row, "col": lax.rem(col + s, ncol)}, device_id_type=MESH
        )
    for r in (above, below):
        for s in range(ncol):
            pl.semaphore_signal(
                barrier, inc=1, device_id={"row": r, "col": lax.rem(col + s, ncol)}, device_id_type=MESH
            )

    for copy in flag_loads:
        copy.wait()
    for b in range(nyb):
        solid = lax.dot_general(
            flags[b].astype(jnp.float32), ex[...], (((0,), (0,)), ((), ())), preferred_element_type=jnp.float32
        )
        mask[b] = 1.0 - solid

    def mask_rows(b, x):
        return jnp.broadcast_to(mask[b, pl.ds(x, 1), :], (YBLK, nz))

    for copy in loads:
        copy.wait()

    @pl.loop(0, ncol)
    def _(d):
        parts = []
        for l in range(lines):
            x = d * lines + l
            parts.append(etop[d, l].astype(jnp.float32) * mask_rows(0, x))
            parts.append(ebot[d, l].astype(jnp.float32) * mask_rows(nyb - 1, x))
        edge = jnp.concatenate(parts, axis=0).astype(jnp.bfloat16)
        halo = jnp.dot(ch[...], edge, preferred_element_type=jnp.float32).astype(jnp.bfloat16)
        hup[d] = halo[: 3 * lines]
        hdown[d] = halo[3 * lines :]

    pl.semaphore_wait(barrier, ncol - 1 + 2 * ncol)

    def halo_copy(src, dst, r, d, way):
        return pltpu.make_async_remote_copy(
            src_ref=src.at[d],
            dst_ref=dst.at[col],
            send_sem=hsend_sem.at[way],
            recv_sem=hrecv_sem.at[way],
            device_id={"row": r, "col": d},
            device_id_type=MESH,
        )

    @pl.loop(0, ncol)
    def _(s):
        d = lax.rem(col + s, ncol)
        halo_copy(hup, hfrom_next, above, d, 0).start()
        halo_copy(hdown, hfrom_prev, below, d, 1).start()

    def line_copy(k, d):
        return pltpu.make_async_remote_copy(
            src_ref=ybuf.at[k, d],
            dst_ref=recv.at[k, col],
            send_sem=send_sem.at[k],
            recv_sem=recv_sem.at[k],
            device_id={"row": row, "col": d},
            device_id_type=MESH,
        )

    @pl.loop(0, lines)
    def _(k):
        pltpu.make_async_copy(field.at[:, k], fbuf.at[k], fsem.at[k]).wait()

        @pl.loop(0, ncol // 2)
        def _(p):
            parts = []
            for h in range(2):
                d = 2 * p + h
                x = d * lines + k
                keep = jnp.concatenate([mask_rows(b, x) for b in range(nyb)], axis=0)
                parts.append((fbuf[k, d].astype(jnp.float32) * keep).astype(jnp.bfloat16))
            out = jnp.dot(fy[...], jnp.concatenate(parts, axis=1), preferred_element_type=jnp.float32)
            ybuf[k, 2 * p] = out[:, :nz].astype(jnp.bfloat16)
            ybuf[k, 2 * p + 1] = out[:, nz:].astype(jnp.bfloat16)

        for flip in order:
            line_copy(k, lax.rem(col + flip, ncol)).start()
        recv[k, col] = ybuf[k, col]

    for copy in late:
        copy.wait()

    def z_filter(block, j):
        near = [block((2 * j + o) % ncol) for o in (-1, 0, 1, 2)]
        out = jnp.dot(jnp.concatenate(near, axis=1), bz[...], preferred_element_type=jnp.float32)
        return out.astype(jnp.bfloat16)

    inner = pl.ds(8, ny - 16)

    def smooth_line(k):
        arrived = recv.at[k, pl.ds(0, ncol - 1)]
        pltpu.make_async_copy(arrived, arrived, recv_sem.at[k]).wait()
        for j in range(ncol // 2):
            filt[k, inner, pl.ds(2 * j * nz, 2 * nz)] = z_filter(lambda c: recv[k, c, inner, :], j)

    @pl.loop(0, lines - 1)
    def _(k):
        smooth_line(k)

        @pl.loop(0, ncol // 2)
        def _(n):
            at = pl.ds(pl.multiple_of(n * (2 * nz), 2 * nz), 2 * nz)
            out = jnp.dot(filt[k, inner, :], dv[:, at], preferred_element_type=jnp.float32)
            der[k, inner, at] = out.astype(jnp.bfloat16)

    last = lines - 1
    smooth_line(last)
    tail[pl.ds(0, ny - 16), :] = filt[last, inner, :]
    for way, ref in ((0, hfrom_next), (1, hfrom_prev)):
        pltpu.make_async_copy(ref, ref, hrecv_sem.at[way]).wait()

    @pl.loop(0, ncol)
    def _(c):
        halo = jnp.concatenate([hfrom_next[c].astype(jnp.float32), hfrom_prev[c].astype(jnp.float32)], axis=0)
        spread = jnp.dot(sp[...], halo.astype(jnp.bfloat16), preferred_element_type=jnp.float32)
        own = []
        for l in range(lines):
            own.append(recv[l, c, pl.ds(0, 8), :].astype(jnp.float32))
            own.append(recv[l, c, pl.ds(ny - 8, 8), :].astype(jnp.float32))
        edges[c] = (jnp.concatenate(own, axis=0) + spread).astype(jnp.bfloat16)

    for j in range(ncol // 2):
        at = pl.ds(2 * j * nz, 2 * nz)
        out = z_filter(lambda c: edges[c], j)
        tail[pl.ds(ny - 16, 16 * lines), at] = out
        for l in range(lines):
            filt[l, pl.ds(0, 8), at] = out[16 * l : 16 * l + 8]
            filt[l, pl.ds(ny - 8, 8), at] = out[16 * l + 8 : 16 * l + 16]

    for k in range(lines):
        sent = ybuf.at[k, pl.ds(0, ncol - 1)]
        pltpu.make_async_copy(sent, sent, send_sem.at[k]).wait()
    for way, ref in ((0, hup), (1, hdown)):
        pltpu.make_async_copy(ref, ref, hsend_sem.at[way]).wait()


def finish_kernel(filt, der, tail, dv, filt_out, der_out, dtail, sem, tail_sem):
    lines, ny, full = filt.shape
    inner = pl.ds(8, ny - 16)
    done = pl.ds(0, lines - 1)
    copies = [
        pltpu.make_async_copy(filt, filt_out, sem.at[0]),
        pltpu.make_async_copy(der.at[done, inner, :], der_out.at[done, inner, :], sem.at[1]),
    ]
    for copy in copies:
        copy.start()
    parts = 2
    width = full // parts
    for h in range(parts):

        @pl.loop(h * (width // 256), (h + 1) * (width // 256))
        def _(n):
            at = pl.ds(pl.multiple_of(n * 256, 256), 256)
            dtail[:, at] = jnp.dot(tail[...], dv[:, at], preferred_element_type=jnp.float32).astype(jnp.bfloat16)

        at = pl.ds(h * width, width)
        rows = ny - 16
        copies.append(
            pltpu.make_async_copy(
                dtail.at[pl.ds(0, rows), at], der_out.at[lines - 1, inner, at], tail_sem.at[h, 2 * lines]
            )
        )
        copies[-1].start()
        for l in range(lines):
            for e, lo in enumerate((0, ny - 8)):
                copies.append(
                    pltpu.make_async_copy(
                        dtail.at[pl.ds(rows + 16 * l + 8 * e, 8), at],
                        der_out.at[l, pl.ds(lo, 8), at],
                        tail_sem.at[h, 2 * l + e],
                    )
                )
                copies[-1].start()
    for copy in copies:
        copy.wait()


def shards(nrow, ncol, field, solid_flags, deriv_matrix):
    nx, ny, nz = field.shape
    nyb, nzb = solid_flags.shape[1:]
    lines = nx // ncol
    full = nz * ncol
    bf16, f32 = jnp.bfloat16, jnp.float32
    order = [s for s in range(1, ncol)]
    out = (lines, ny, full)
    any_spec = pl.BlockSpec(memory_space=pl.ANY)
    vmem = pl.BlockSpec(memory_space=pltpu.VMEM)
    consts = [
        jnp.asarray(y_matrix(ny), bf16),
        jnp.asarray(halo_matrix(lines), bf16),
        jnp.asarray(spread_matrix(lines), bf16),
        jnp.asarray(z_matrix(nz), bf16),
        jnp.asarray(expand_matrix(nzb), f32),
    ]
    tail = ny - 16 + 16 * lines
    held = pl.pallas_call(
        functools.partial(exchange_kernel, nrow, ncol, order),
        name="exchange",
        out_shape=[pltpu.VMEM(shape, bf16) for shape in (out, out, (tail, full), (full, full))],
        in_specs=[any_spec, any_spec, any_spec, any_spec, any_spec, any_spec, any_spec, any_spec],
        out_specs=[vmem] * 4,
        scratch_shapes=[
            pltpu.VMEM((lines, ncol, ny, nz), bf16),
            pltpu.VMEM((ncol, lines, 8, nz), bf16),
            pltpu.VMEM((ncol, lines, 8, nz), bf16),
            pltpu.VMEM((nyb, nx, nz), f32),
            pltpu.VMEM((lines, ncol, ny, nz), bf16),
            pltpu.VMEM((lines, ncol, ny, nz), bf16),
            pltpu.VMEM((ncol, 3 * lines, nz), bf16),
            pltpu.VMEM((ncol, 3 * lines, nz), bf16),
            pltpu.VMEM((ncol, 3 * lines, nz), bf16),
            pltpu.VMEM((ncol, 3 * lines, nz), bf16),
            pltpu.VMEM((ncol, 16 * lines, nz), bf16),
            *[pltpu.VMEM(c.shape, c.dtype) for c in consts],
            pltpu.VMEM((nyb, nzb, nx), jnp.int32),
            pltpu.SemaphoreType.DMA((9,)),
            pltpu.SemaphoreType.DMA((lines,)),
            pltpu.SemaphoreType.DMA((lines,)),
            pltpu.SemaphoreType.DMA((lines,)),
            pltpu.SemaphoreType.DMA((2,)),
            pltpu.SemaphoreType.DMA((2,)),
        ],
        compiler_params=pltpu.CompilerParams(
            collective_id=0, has_side_effects=True, vmem_limit_bytes=45 * 1024 * 1024
        ),
    )(
        field.reshape(ncol, lines, ny, nz),
        jnp.transpose(solid_flags, (1, 2, 0)),
        deriv_matrix,
        *consts,
    )
    return pl.pallas_call(
        finish_kernel,
        name="finish",
        out_shape=[jax.ShapeDtypeStruct(out, bf16)] * 2,
        in_specs=[vmem] * 4,
        out_specs=[any_spec, any_spec],
        scratch_shapes=[
            pltpu.VMEM((tail, full), bf16),
            pltpu.SemaphoreType.DMA((2,)),
            pltpu.SemaphoreType.DMA((2, 2 * lines + 1)),
        ],
        compiler_params=pltpu.CompilerParams(vmem_limit_bytes=8 * 1024 * 1024),
    )(*held)


def solution(mesh):
    in_specs = (P(None, "row", "col"), P(None, "row", "col"), P())
    out_specs = (P("col", "row", None), P("col", "row", None))
    body = functools.partial(shards, mesh.shape["row"], mesh.shape["col"])
    return jax.shard_map(body, mesh=mesh, in_specs=in_specs, out_specs=out_specs, check_vma=False)
```

time: 137 us -> 71.4 us (0.52); the launches traced: 135 us -> 71.3 us
  Pallas kernels: 0 us -> 70.6 us
  waiting for transfers between devices: 52.8 us -> 0 us
  other arithmetic: 29 us -> 0 us
  starting transfers between devices: 22.3 us -> 0 us
  local copies, waits for them, and re-layouts: 21 us -> 0 us
  matrix products: 9.39 us -> 0 us
    pallas_call x0 -> x2, Pallas kernels: none -> 70.6 us  [the longest x1 65.9 us: shards(): pl.pallas_call(functools.partial(exchange_kernel, nrow, ncol, order), nam...]
    all_to_all x2 -> x0, waiting for transfers between devices: 50.4 us -> none  [grouped_exchange(): lax.all_to_all(group, axis, split_axis=split_dim, concat_axis=concat_dim,...]
    convert_element_type x3 -> x0, other arithmetic: 22.9 us -> none  [the longest x1 11.9 us: prepare(): return smooth_padded(padded, 2, full).astype(jnp.bfloat16)]
    all_to_all x2 -> x0, starting transfers between devices: 14.8 us -> none  [grouped_exchange(): lax.all_to_all(group, axis, split_axis=split_dim, concat_axis=concat_dim,...]
    dot_general x2 -> x0, matrix products: 9.39 us -> none  [finish(): jnp.dot(flat, deriv_matrix, preferred_element_type=jnp.float32)]
    slice x6 -> x0, local copies, waits for them, and re-layouts: 8.74 us -> none  [the longest x3 8.5 us: grouped_exchange(): lax.slice_in_dim(a, k * (items // count), (k + 1) * (items // count), axi...]
    ppermute x2 -> x0, starting transfers between devices: 7.49 us -> none  [the longest x1 5.38 us: with_halo(): lax.ppermute(lax.slice_in_dim(block, 0, width, axis=dim), axis, backward)]
    unnamed x7 -> x0, local copies, waits for them, and re-layouts: 6.91 us -> none
  transfers between devices with their start and end apart: 4 -> 0, of which waited for: 3 -> 0; matrix products, arithmetic and copies ran while one was open for 5% -> 0% of each run, Pallas kernels for 0% -> 0%
where the time goes in v1:
time: 71.4 us; the launch traced here: 71.3 us
  Pallas kernels  70.6 us (99%)
    pallas_call x1, Pallas kernels, shards(): pl.pallas_call(functools.partial(exchange_kernel, nrow, ncol, order), nam...  65.9 us
    pallas_call x1, Pallas kernels, shards(): pl.pallas_call(finish_kernel, name='finish', out_shape=[jax.ShapeDtypeStr...  4.71 us

profile of v1, /device:TPU:1, one launch (start us, length us, event | category | flops | bytes accessed | tf_op | source)
XLA Modules:
  0.0 71.3 jit_solution(4855209016126075570)
XLA Ops:
  0.6 65.9 %exchange.1 = (bf16[8,128,2048]{2,1,0:T(8,128)(2,1)S(1)}, bf16[8,128,2048]{2,1,0:T(8,128)(2,1)S(1)}, bf16[240,2048]{1,0:T(8,128)(2,1)S(1)}, bf16[2048,2048]{1,0:T(8,128)(2,1)S(1)}) custom-call(bf16[16,8,128,128]{3,2,1,0:T(8,128)(2,1)} %bitcast.2, s32[16,8,128]{2,1,0:T(8,128)} %bitcast.3, bf16[2048,2048]{1,0:T(8,128)(2,1)} %dmat.1, ...), custom_call_target="tpu_custom_call" | custom-call | tf_op jit(solution)/shard_map/exchange/pallas_call | solution.py:300
  66.6 4.7 %finish.1 = (bf16[8,128,2048]{2,1,0:T(8,128)(2,1)}, bf16[8,128,2048]{2,1,0:T(8,128)(2,1)}) custom-call(bf16[8,128,2048]{2,1,0:T(8,128)(2,1)S(1)} %get-tuple-element.6.filt, bf16[8,128,2048]{2,1,0:T(8,128)(2,1)S(1)} %get-tuple-element.7.der, bf16[240,2048]{1,0:T(8,128)(2,1)S(1)} %get-tuple-element.8.tail, bf16[2048,2048]{1,0:T(8,128)(2,1)S(1)} %get-tuple-element.9.dv), custom_call_target="tpu_custom_call" | custom-call | tf_op jit(solution)/shard_map/finish/pallas_call | solution.py:336

commit v2 on v1

v2 whole, which is shorter than its diff:
```python
import functools

import jax
import jax.numpy as jnp
import numpy as np
from jax import lax
from jax.experimental import pallas as pl
from jax.experimental.pallas import tpu as pltpu
from jax.sharding import PartitionSpec as P

MESH = pl.DeviceIdType.MESH
YBLK = 8
ZBLK = 16
TAPS = {-3: 1.0, -2: -6.0, -1: 15.0, 0: 44.0, 1: 15.0, 2: -6.0, 3: 1.0}


def y_matrix(ny):
    out = np.zeros((ny, ny), np.float32)
    for r in range(ny):
        for o, tap in TAPS.items():
            if 0 <= r + o < ny:
                out[r, r + o] = tap / 64.0
    return out


def halo_matrix(lines):
    up = np.zeros((lines * 3, lines * 16), np.float32)
    down = np.zeros((lines * 3, lines * 16), np.float32)
    for l in range(lines):
        for j in range(3):
            for q in range(3):
                o = q - (j - 3)
                if o in TAPS:
                    up[l * 3 + j, l * 16 + q] = TAPS[o] / 64.0
                o = (q - 3) - j
                if o in TAPS:
                    down[l * 3 + j, l * 16 + 8 + 5 + q] = TAPS[o] / 64.0
    return np.concatenate([up, down], axis=0)


def spread_matrix(lines):
    out = np.zeros((lines * 16, lines * 6), np.float32)
    for l in range(lines):
        for j in range(3):
            out[l * 16 + 8 + 5 + j, l * 3 + j] = 1.0
            out[l * 16 + j, lines * 3 + l * 3 + j] = 1.0
    return out


def z_matrix(nz):
    out = np.zeros((4 * nz, 2 * nz), np.float32)
    for c in range(2 * nz):
        for o, tap in TAPS.items():
            out[nz + c + o, c] = tap / 64.0
    return out


def expand_matrix(nyb, nzb):
    return np.kron(np.eye(nyb, dtype=np.float32), np.repeat(np.eye(nzb, dtype=np.float32), ZBLK, axis=1))


def exchange_kernel(
    nrow, ncol, order,
    field, flags_in, dmat, fy_in, ch_in, sp_in, bz_in, ex_in,
    filt, der, tail, dv,
    fbuf, etop, ebot, mask, mbuf, ybuf, recv, hup, hdown, hfrom_next, hfrom_prev, spread, edges,
    fy, ch, sp, bz, ex, flags,
    in_sem, fsem, send_sem, recv_sem, hsend_sem, hrecv_sem,
):
    row, col = lax.axis_index("row"), lax.axis_index("col")
    above, below = lax.rem(row + nrow - 1, nrow), lax.rem(row + 1, nrow)
    lines, ny, nz = fbuf.shape[0], fbuf.shape[2], fbuf.shape[3]
    nyb = ny // YBLK
    bf16, f32 = jnp.bfloat16, jnp.float32

    flag_loads = [
        pltpu.make_async_copy(flags_in, flags, in_sem.at[7]),
        pltpu.make_async_copy(ex_in, ex, in_sem.at[8]),
        pltpu.make_async_copy(fy_in, fy, in_sem.at[3]),
    ]
    field_loads = [pltpu.make_async_copy(field.at[:, k], fbuf.at[k], fsem.at[k]) for k in range(lines)]
    edge_loads = [
        pltpu.make_async_copy(field.at[:, :, pl.ds(0, 8), :], etop, in_sem.at[0]),
        pltpu.make_async_copy(field.at[:, :, pl.ds(ny - 8, 8), :], ebot, in_sem.at[1]),
        pltpu.make_async_copy(ch_in, ch, in_sem.at[2]),
    ]
    late = [
        pltpu.make_async_copy(sp_in, sp, in_sem.at[4]),
        pltpu.make_async_copy(bz_in, bz, in_sem.at[5]),
        pltpu.make_async_copy(dmat, dv, in_sem.at[6]),
    ]
    for copy in [*flag_loads, field_loads[0], *edge_loads, *field_loads[1:], *late]:
        copy.start()

    barrier = pltpu.get_barrier_semaphore()
    for s in range(1, ncol):
        pl.semaphore_signal(
            barrier, inc=1, device_id={"row": row, "col": lax.rem(col + s, ncol)}, device_id_type=MESH
        )
    for r in (above, below):
        for s in range(ncol):
            pl.semaphore_signal(
                barrier, inc=1, device_id={"row": r, "col": lax.rem(col + s, ncol)}, device_id_type=MESH
            )

    for copy in flag_loads:
        copy.wait()
    per_line = flags[...].astype(f32).T.astype(bf16)
    for n in range(nyb // 4):
        solid = jnp.dot(per_line, ex[:, pl.ds(n * 4 * nz, 4 * nz)], preferred_element_type=f32)
        for b in range(4):
            mask[4 * n + b] = 1.0 - solid[:, b * nz : (b + 1) * nz]

    def mask_rows(b, x):
        return jnp.broadcast_to(mask[b, pl.ds(x, 1), :], (YBLK, nz))

    def filter_lines(k):
        for d in range(ncol):
            x = d * lines + k
            keep = jnp.concatenate([mask_rows(b, x) for b in range(nyb)], axis=0)
            mbuf[:, pl.ds(d * nz, nz)] = (fbuf[k, d].astype(f32) * keep).astype(bf16)
        for n in range(ncol // 4):
            out = jnp.dot(fy[...], mbuf[:, pl.ds(n * 4 * nz, 4 * nz)], preferred_element_type=f32)
            for i in range(4):
                ybuf[k, 4 * n + i] = out[:, i * nz : (i + 1) * nz].astype(bf16)

    def send_lines(k):
        for a, b, c in order:
            d = (lax.rem(col // 8 + a, 2) * 4 + lax.rem(col // 2 + b, 4)) * 2 + lax.rem(col + c, 2)
            pltpu.make_async_remote_copy(
                src_ref=ybuf.at[k, d],
                dst_ref=recv.at[k, col],
                send_sem=send_sem.at[k],
                recv_sem=recv_sem.at[k],
                device_id={"row": row, "col": d},
                device_id_type=MESH,
            ).start()
        recv[k, col] = ybuf[k, col]

    def halo_copy(src, dst, r, d, way):
        return pltpu.make_async_remote_copy(
            src_ref=src.at[d],
            dst_ref=dst.at[col],
            send_sem=hsend_sem.at[way],
            recv_sem=hrecv_sem.at[way],
            device_id={"row": r, "col": d},
            device_id_type=MESH,
        )

    field_loads[0].wait()
    filter_lines(0)
    pl.semaphore_wait(barrier, ncol - 1 + 2 * ncol)
    send_lines(0)

    for copy in edge_loads:
        copy.wait()
    for d in range(ncol):
        parts = []
        for l in range(lines):
            x = d * lines + l
            parts.append(etop[d, l].astype(f32) * mask_rows(0, x))
            parts.append(ebot[d, l].astype(f32) * mask_rows(nyb - 1, x))
        mbuf[:, pl.ds(d * nz, nz)] = jnp.concatenate(parts, axis=0).astype(bf16)
    for n in range(ncol // 4):
        halo = jnp.dot(ch[...], mbuf[:, pl.ds(n * 4 * nz, 4 * nz)], preferred_element_type=f32).astype(bf16)
        for i in range(4):
            hup[4 * n + i] = halo[: 3 * lines, i * nz : (i + 1) * nz]
            hdown[4 * n + i] = halo[3 * lines :, i * nz : (i + 1) * nz]

    @pl.loop(0, ncol)
    def _(s):
        d = lax.rem(col + s, ncol)
        halo_copy(hup, hfrom_next, above, d, 0).start()
        halo_copy(hdown, hfrom_prev, below, d, 1).start()

    @pl.loop(1, lines)
    def _(k):
        pltpu.make_async_copy(field.at[:, k], fbuf.at[k], fsem.at[k]).wait()
        filter_lines(k)
        send_lines(k)

    for copy in late:
        copy.wait()

    def z_filter(block, j):
        near = [block((2 * j + o) % ncol) for o in (-1, 0, 1, 2)]
        out = jnp.dot(jnp.concatenate(near, axis=1), bz[...], preferred_element_type=f32)
        return out.astype(bf16)

    def arrive(k):
        arrived = recv.at[k, pl.ds(0, ncol - 1)]
        pltpu.make_async_copy(arrived, arrived, recv_sem.at[k]).wait()

    inner = pl.ds(8, ny - 16)
    last = lines - 1

    @pl.loop(0, last)
    def _(k):
        arrive(k)
        for j in range(ncol // 2):
            filt[k, inner, pl.ds(2 * j * nz, 2 * nz)] = z_filter(lambda c: recv[k, c, inner, :], j)

        @pl.loop(0, ncol // 2)
        def _(n):
            at = pl.ds(pl.multiple_of(n * (2 * nz), 2 * nz), 2 * nz)
            der[k, inner, at] = jnp.dot(filt[k, inner, :], dv[:, at], preferred_element_type=f32).astype(bf16)

    for way, ref in ((0, hfrom_next), (1, hfrom_prev)):
        pltpu.make_async_copy(ref, ref, hrecv_sem.at[way]).wait()
    for n in range(ncol // 4):
        halo = [
            jnp.concatenate([hfrom_next[c].astype(f32), hfrom_prev[c].astype(f32)], axis=0).astype(bf16)
            for c in range(4 * n, 4 * n + 4)
        ]
        out = jnp.dot(sp[...], jnp.concatenate(halo, axis=1), preferred_element_type=f32)
        for i in range(4):
            spread[4 * n + i] = out[:, i * nz : (i + 1) * nz]
    for c in range(ncol):
        own = []
        for l in range(last):
            own.append(recv[l, c, pl.ds(0, 8), :].astype(f32))
            own.append(recv[l, c, pl.ds(ny - 8, 8), :].astype(f32))
        edges[c] = (jnp.concatenate(own, axis=0) + spread[c, pl.ds(0, 16 * last), :]).astype(bf16)
    for j in range(ncol // 2):
        at = pl.ds(2 * j * nz, 2 * nz)
        out = z_filter(lambda c: edges[c], j)
        tail[pl.ds(ny, 16 * last), at] = out
        for l in range(last):
            filt[l, pl.ds(0, 8), at] = out[16 * l : 16 * l + 8]
            filt[l, pl.ds(ny - 8, 8), at] = out[16 * l + 8 : 16 * l + 16]

    arrive(last)
    for c in range(ncol):
        for lo, at in ((0, 0), (ny - 8, 8)):
            rows = pl.ds(lo, 8)
            recv[last, c, rows, :] = (
                recv[last, c, rows, :].astype(f32) + spread[c, pl.ds(16 * last + at, 8), :]
            ).astype(bf16)
    for j in range(ncol // 2):
        at = pl.ds(2 * j * nz, 2 * nz)
        out = z_filter(lambda c: recv[last, c], j)
        tail[pl.ds(0, ny), at] = out
        filt[last, :, at] = out

    for k in range(lines):
        sent = ybuf.at[k, pl.ds(0, ncol - 1)]
        pltpu.make_async_copy(sent, sent, send_sem.at[k]).wait()
    for way, ref in ((0, hup), (1, hdown)):
        pltpu.make_async_copy(ref, ref, hsend_sem.at[way]).wait()


def finish_kernel(filt, der, tail, dv, filt_out, der_out, dtail, sem, tail_sem):
    lines, ny, full = filt.shape
    inner = pl.ds(8, ny - 16)
    done = pl.ds(0, lines - 1)
    copies = [
        pltpu.make_async_copy(filt, filt_out, sem.at[0]),
        pltpu.make_async_copy(der.at[done, inner, :], der_out.at[done, inner, :], sem.at[1]),
    ]
    for copy in copies:
        copy.start()
    parts = 2
    width = full // parts
    for h in range(parts):
        at = pl.ds(h * width, width)
        dtail[:, at] = jnp.dot(tail[...], dv[:, at], preferred_element_type=jnp.float32).astype(jnp.bfloat16)
        copies.append(
            pltpu.make_async_copy(
                dtail.at[pl.ds(0, ny), at], der_out.at[lines - 1, :, at], tail_sem.at[h, 2 * lines - 2]
            )
        )
        copies[-1].start()
        for l in range(lines - 1):
            for e, lo in enumerate((0, ny - 8)):
                copies.append(
                    pltpu.make_async_copy(
                        dtail.at[pl.ds(ny + 16 * l + 8 * e, 8), at],
                        der_out.at[l, pl.ds(lo, 8), at],
                        tail_sem.at[h, 2 * l + e],
                    )
                )
                copies[-1].start()
    for copy in copies:
        copy.wait()


def shards(nrow, ncol, field, solid_flags, deriv_matrix):
    nx, ny, nz = field.shape
    nyb, nzb = solid_flags.shape[1:]
    lines = nx // ncol
    full = nz * ncol
    bf16, f32 = jnp.bfloat16, jnp.float32
    along_x = [(1, b, c) for b in (2, 1, 3, 0) for c in (0, 1)]
    along_y = [(0, b, c) for b in (2, 1, 3) for c in (0, 1)] + [(0, 0, 1)]
    order = [step for pair in zip(along_x, along_y) for step in pair] + along_x[len(along_y) :]
    out = (lines, ny, full)
    any_spec = pl.BlockSpec(memory_space=pl.ANY)
    vmem = pl.BlockSpec(memory_space=pltpu.VMEM)
    consts = [
        jnp.asarray(y_matrix(ny), bf16),
        jnp.asarray(halo_matrix(lines), bf16),
        jnp.asarray(spread_matrix(lines), bf16),
        jnp.asarray(z_matrix(nz), bf16),
        jnp.asarray(expand_matrix(nyb, nzb), bf16),
    ]
    tail = ny + 16 * (lines - 1)
    held = pl.pallas_call(
        functools.partial(exchange_kernel, nrow, ncol, order),
        name="exchange",
        out_shape=[pltpu.VMEM(shape, bf16) for shape in (out, out, (tail, full), (full, full))],
        in_specs=[any_spec, any_spec, any_spec, any_spec, any_spec, any_spec, any_spec, any_spec],
        out_specs=[vmem] * 4,
        scratch_shapes=[
            pltpu.VMEM((lines, ncol, ny, nz), bf16),
            pltpu.VMEM((ncol, lines, 8, nz), bf16),
            pltpu.VMEM((ncol, lines, 8, nz), bf16),
            pltpu.VMEM((nyb, nx, nz), f32),
            pltpu.VMEM((ny, full), bf16),
            pltpu.VMEM((lines, ncol, ny, nz), bf16),
            pltpu.VMEM((lines, ncol, ny, nz), bf16),
            pltpu.VMEM((ncol, 3 * lines, nz), bf16),
            pltpu.VMEM((ncol, 3 * lines, nz), bf16),
            pltpu.VMEM((ncol, 3 * lines, nz), bf16),
            pltpu.VMEM((ncol, 3 * lines, nz), bf16),
            pltpu.VMEM((ncol, 16 * lines, nz), f32),
            pltpu.VMEM((ncol, 16 * (lines - 1), nz), bf16),
            *[pltpu.VMEM(c.shape, c.dtype) for c in consts],
            pltpu.VMEM((nyb * nzb, nx), jnp.int32),
            pltpu.SemaphoreType.DMA((9,)),
            pltpu.SemaphoreType.DMA((lines,)),
            pltpu.SemaphoreType.DMA((lines,)),
            pltpu.SemaphoreType.DMA((lines,)),
            pltpu.SemaphoreType.DMA((2,)),
            pltpu.SemaphoreType.DMA((2,)),
        ],
        compiler_params=pltpu.CompilerParams(
            collective_id=0, has_side_effects=True, vmem_limit_bytes=45 * 1024 * 1024
        ),
    )(
        field.reshape(ncol, lines, ny, nz),
        jnp.transpose(solid_flags, (1, 2, 0)).reshape(nyb * nzb, nx),
        deriv_matrix,
        *consts,
    )
    return pl.pallas_call(
        finish_kernel,
        name="finish",
        out_shape=[jax.ShapeDtypeStruct(out, bf16)] * 2,
        in_specs=[vmem] * 4,
        out_specs=[any_spec, any_spec],
        scratch_shapes=[
            pltpu.VMEM((tail, full), bf16),
            pltpu.SemaphoreType.DMA((2,)),
            pltpu.SemaphoreType.DMA((2, 2 * lines - 1)),
        ],
        compiler_params=pltpu.CompilerParams(vmem_limit_bytes=8 * 1024 * 1024),
    )(*held)


def solution(mesh):
    in_specs = (P(None, "row", "col"), P(None, "row", "col"), P())
    out_specs = (P("col", "row", None), P("col", "row", None))
    body = functools.partial(shards, mesh.shape["row"], mesh.shape["col"])
    return jax.shard_map(body, mesh=mesh, in_specs=in_specs, out_specs=out_specs, check_vma=False)
```

time: 71.4 us -> 66.5 us (0.931)
  Pallas kernels: 70.6 us -> 65.8 us
    pallas_call x1, Pallas kernels: 65.9 us -> 62.3 us  [shards(): pl.pallas_call(functools.partial(exchange_kernel, nrow, ncol, order), nam...]
    pallas_call x1, Pallas kernels: 4.71 us -> 3.52 us  [shards(): pl.pallas_call(finish_kernel, name='finish', out_shape=[jax.ShapeDtypeStr...]
where the time goes in v2:
time: 66.5 us; the launch traced here: 66.4 us
  Pallas kernels  65.8 us (99%)
    pallas_call x1, Pallas kernels, shards(): pl.pallas_call(functools.partial(exchange_kernel, nrow, ncol, order), nam...  62.3 us
    pallas_call x1, Pallas kernels, shards(): pl.pallas_call(finish_kernel, name='finish', out_shape=[jax.ShapeDtypeStr...  3.52 us

profile of v2, /device:TPU:1, one launch (start us, length us, event | category | flops | bytes accessed | tf_op | source)
XLA Modules:
  0.0 66.4 jit_solution(16097490257299627909)
XLA Ops:
  0.6 62.3 %exchange.1 = (bf16[8,128,2048]{2,1,0:T(8,128)(2,1)S(1)}, bf16[8,128,2048]{2,1,0:T(8,128)(2,1)S(1)}, bf16[240,2048]{1,0:T(8,128)(2,1)S(1)}, bf16[2048,2048]{1,0:T(8,128)(2,1)S(1)}) custom-call(bf16[16,8,128,128]{3,2,1,0:T(8,128)(2,1)} %bitcast.4, s32[128,128]{1,0:T(8,128)} %bitcast.5, bf16[2048,2048]{1,0:T(8,128)(2,1)} %dmat.1, ...), custom_call_target="tpu_custom_call" | custom-call | tf_op jit(solution)/shard_map/exchange/pallas_call | solution.py:307
  62.9 3.5 %finish.1 = (bf16[8,128,2048]{2,1,0:T(8,128)(2,1)}, bf16[8,128,2048]{2,1,0:T(8,128)(2,1)}) custom-call(bf16[8,128,2048]{2,1,0:T(8,128)(2,1)S(1)} %get-tuple-element.6.filt, bf16[8,128,2048]{2,1,0:T(8,128)(2,1)S(1)} %get-tuple-element.7.der, bf16[240,2048]{1,0:T(8,128)(2,1)S(1)} %get-tuple-element.8.tail, bf16[2048,2048]{1,0:T(8,128)(2,1)S(1)} %get-tuple-element.9.dv), custom_call_target="tpu_custom_call" | custom-call | tf_op jit(solution)/shard_map/finish/pallas_call | solution.py:345

commit v3 on v2

--- a/solution.py
+++ b/solution.py
@@ -9,6 +9,8 @@
 from jax.sharding import PartitionSpec as P
 
 MESH = pl.DeviceIdType.MESH
+GATE = 1
+EARLY = 5
 YBLK = 8
 ZBLK = 16
 TAPS = {-3: 1.0, -2: -6.0, -1: 15.0, 0: 44.0, 1: 15.0, 2: -6.0, 3: 1.0}
@@ -65,7 +67,7 @@
     filt, der, tail, dv,
     fbuf, etop, ebot, mask, mbuf, ybuf, recv, hup, hdown, hfrom_next, hfrom_prev, spread, edges,
     fy, ch, sp, bz, ex, flags,
-    in_sem, fsem, send_sem, recv_sem, hsend_sem, hrecv_sem,
+    in_sem, fsem, send_sem, recv_sem, hsend_sem, hrecv_sem, joined, rows_in,
 ):
     row, col = lax.axis_index("row"), lax.axis_index("col")
     above, below = lax.rem(row + nrow - 1, nrow), lax.rem(row + 1, nrow)
@@ -94,14 +96,11 @@
 
     barrier = pltpu.get_barrier_semaphore()
     for s in range(1, ncol):
-        pl.semaphore_signal(
-            barrier, inc=1, device_id={"row": row, "col": lax.rem(col + s, ncol)}, device_id_type=MESH
-        )
-    for r in (above, below):
-        for s in range(ncol):
-            pl.semaphore_signal(
-                barrier, inc=1, device_id={"row": r, "col": lax.rem(col + s, ncol)}, device_id_type=MESH
-            )
+        d = lax.rem(col + s, ncol)
+
+        @pl.when(d != GATE)
+        def _():
+            pl.semaphore_signal(barrier, inc=1, device_id={"row": row, "col": d}, device_id_type=MESH)
 
     for copy in flag_loads:
         copy.wait()
@@ -149,8 +148,25 @@
 
     field_loads[0].wait()
     filter_lines(0)
-    pl.semaphore_wait(barrier, ncol - 1 + 2 * ncol)
+
+    @pl.when(col != GATE)
+    def _():
+        pl.semaphore_wait(barrier, ncol - 1)
+        pl.semaphore_signal(joined, inc=1, device_id={"row": row, "col": GATE}, device_id_type=MESH)
+
+    @pl.when(col == GATE)
+    def _():
+        pl.semaphore_wait(joined, ncol - 1)
+        for r in (above, below):
+            pl.semaphore_signal(barrier, inc=1, device_id={"row": r, "col": GATE}, device_id_type=MESH)
+
     send_lines(0)
+
+    @pl.loop(1, EARLY)
+    def _(k):
+        pltpu.make_async_copy(field.at[:, k], fbuf.at[k], fsem.at[k]).wait()
+        filter_lines(k)
+        send_lines(k)
 
     for copy in edge_loads:
         copy.wait()
@@ -167,13 +183,25 @@
             hup[4 * n + i] = halo[: 3 * lines, i * nz : (i + 1) * nz]
             hdown[4 * n + i] = halo[3 * lines :, i * nz : (i + 1) * nz]
 
+    @pl.when(col == GATE)
+    def _():
+        pl.semaphore_wait(barrier, 2)
+        for s in range(1, ncol):
+            pl.semaphore_signal(
+                rows_in, inc=1, device_id={"row": row, "col": lax.rem(col + s, ncol)}, device_id_type=MESH
+            )
+
+    @pl.when(col != GATE)
+    def _():
+        pl.semaphore_wait(rows_in, 1)
+
     @pl.loop(0, ncol)
     def _(s):
         d = lax.rem(col + s, ncol)
         halo_copy(hup, hfrom_next, above, d, 0).start()
         halo_copy(hdown, hfrom_prev, below, d, 1).start()
 
-    @pl.loop(1, lines)
+    @pl.loop(EARLY, lines)
     def _(k):
         pltpu.make_async_copy(field.at[:, k], fbuf.at[k], fsem.at[k]).wait()
         filter_lines(k)
@@ -332,6 +360,8 @@
             pltpu.SemaphoreType.DMA((lines,)),
             pltpu.SemaphoreType.DMA((2,)),
             pltpu.SemaphoreType.DMA((2,)),
+            pltpu.SemaphoreType.REGULAR,
+            pltpu.SemaphoreType.REGULAR,
         ],
         compiler_params=pltpu.CompilerParams(
             collective_id=0, has_side_effects=True, vmem_limit_bytes=45 * 1024 * 1024

time: 66.5 us -> 62.8 us (0.944)
  the two profiles are of different devices: /device:TPU:1 before, /device:TPU:33 now
where the time goes in v3:
time: 62.8 us
  Pallas kernels  62.1 us (99%)
  between operations  0.64 us (1%)
    pallas_call x1, Pallas kernels, shards(): pl.pallas_call(functools.partial(exchange_kernel, nrow, ncol, order), nam...  58.6 us
    pallas_call x1, Pallas kernels, shards(): pl.pallas_call(finish_kernel, name='finish', out_shape=[jax.ShapeDtypeStr...  3.52 us

profile of v3, /device:TPU:33, one launch (start us, length us, event | category | flops | bytes accessed | tf_op | source)
XLA Modules:
  0.0 62.8 jit_solution(6360630554440177206)
XLA Ops:
  0.6 58.6 %exchange.1 = (bf16[8,128,2048]{2,1,0:T(8,128)(2,1)S(1)}, bf16[8,128,2048]{2,1,0:T(8,128)(2,1)S(1)}, bf16[240,2048]{1,0:T(8,128)(2,1)S(1)}, bf16[2048,2048]{1,0:T(8,128)(2,1)S(1)}) custom-call(bf16[16,8,128,128]{3,2,1,0:T(8,128)(2,1)} %bitcast.4, s32[128,128]{1,0:T(8,128)} %bitcast.5, bf16[2048,2048]{1,0:T(8,128)(2,1)} %dmat.1, ...), custom_call_target="tpu_custom_call" | custom-call | tf_op jit(solution)/shard_map/exchange/pallas_call | solution.py:335
  59.2 3.5 %finish.1 = (bf16[8,128,2048]{2,1,0:T(8,128)(2,1)}, bf16[8,128,2048]{2,1,0:T(8,128)(2,1)}) custom-call(bf16[8,128,2048]{2,1,0:T(8,128)(2,1)S(1)} %get-tuple-element.6.filt, bf16[8,128,2048]{2,1,0:T(8,128)(2,1)S(1)} %get-tuple-element.7.der, bf16[240,2048]{1,0:T(8,128)(2,1)S(1)} %get-tuple-element.8.tail, bf16[2048,2048]{1,0:T(8,128)(2,1)S(1)} %get-tuple-element.9.dv), custom_call_target="tpu_custom_call" | custom-call | tf_op jit(solution)/shard_map/finish/pallas_call | solution.py:375

commit v4 on v3

--- a/solution.py
+++ b/solution.py
@@ -9,7 +9,7 @@
 from jax.sharding import PartitionSpec as P
 
 MESH = pl.DeviceIdType.MESH
-GATE = 1
+GATE = 15
 EARLY = 5
 YBLK = 8
 ZBLK = 16

time: 62.8 us -> 61.8 us (0.984)
  the two profiles are of different devices: /device:TPU:33 before, /device:TPU:1 now
where the time goes in v4:
time: 61.8 us; the launch traced here: 61.7 us
  Pallas kernels  61.1 us (99%)
  between operations  0.64 us (1%)
    pallas_call x1, Pallas kernels, shards(): pl.pallas_call(functools.partial(exchange_kernel, nrow, ncol, order), nam...  57.5 us
    pallas_call x1, Pallas kernels, shards(): pl.pallas_call(finish_kernel, name='finish', out_shape=[jax.ShapeDtypeStr...  3.52 us

profile of v4, /device:TPU:1, one launch (start us, length us, event | category | flops | bytes accessed | tf_op | source)
XLA Modules:
  0.0 61.7 jit_solution(10121838543375301207)
XLA Ops:
  0.6 57.5 %exchange.1 = (bf16[8,128,2048]{2,1,0:T(8,128)(2,1)S(1)}, bf16[8,128,2048]{2,1,0:T(8,128)(2,1)S(1)}, bf16[240,2048]{1,0:T(8,128)(2,1)S(1)}, bf16[2048,2048]{1,0:T(8,128)(2,1)S(1)}) custom-call(bf16[16,8,128,128]{3,2,1,0:T(8,128)(2,1)} %bitcast.4, s32[128,128]{1,0:T(8,128)} %bitcast.5, bf16[2048,2048]{1,0:T(8,128)(2,1)} %dmat.1, ...), custom_call_target="tpu_custom_call" | custom-call | tf_op jit(solution)/shard_map/exchange/pallas_call | solution.py:335
  58.2 3.5 %finish.1 = (bf16[8,128,2048]{2,1,0:T(8,128)(2,1)}, bf16[8,128,2048]{2,1,0:T(8,128)(2,1)}) custom-call(bf16[8,128,2048]{2,1,0:T(8,128)(2,1)S(1)} %get-tuple-element.6.filt, bf16[8,128,2048]{2,1,0:T(8,128)(2,1)S(1)} %get-tuple-element.7.der, bf16[240,2048]{1,0:T(8,128)(2,1)S(1)} %get-tuple-element.8.tail, bf16[2048,2048]{1,0:T(8,128)(2,1)S(1)} %get-tuple-element.9.dv), custom_call_target="tpu_custom_call" | custom-call | tf_op jit(solution)/shard_map/finish/pallas_call | solution.py:375
